TPU v7x, 32 devices: a whole 2x2x4 slice. The times are simulated.
32 devices in a mesh: wide: 8 (over y, x, core), narrow: 4 (over z).
Axes of the slice: x: 2, y: 2, z: 4, core: 2. Of those that a mesh axis runs over, the one named last changes fastest.
Arguments:
- panels: float32 [64, 512, 512], P('wide', 'narrow'), may hold values from -0.6 to 0.6
- factors: float32 [16, 512, 512], P('wide', 'narrow'), may hold values from -2 to 2
- member: int32 [16, 4], replicated, may hold values from 0 to 63, as said below
- target: int32 [16, 10], replicated, may hold values from 0 to 7
- ancestors: float32 [8, 512, 512], P('wide', 'narrow'), may hold values from -6 to 6
Outputs:
- updated: float32 [8, 512, 512], P('wide', 'narrow')
Inputs may be any that keep to these rules, and one draw needn't show every extreme that they name: `member`: the blocks of supernode s are 4 distinct indices in [(s // 2) * 8, (s // 2 + 1) * 8); every block belongs to exactly one supernode.
All inputs are finite; a program needn't handle non-finite values.
Results may differ from a plain program's by a relative error of at most 0.0003.
Values sent between devices are 32-bit elements; how exact they have to be, the bound alone decides.
A program may use at most 128 MiB of HBM per device.

v0:
```python
import functools

import jax
import jax.numpy as jnp
from jax import lax
from jax.experimental import pallas as pl
from jax.experimental.pallas import tpu as pltpu
from jax.sharding import PartitionSpec as P

MESH = pl.DeviceIdType.MESH
CORES = 2
ROWS_DOT = (((1,), (1,)), ((), ()))
COLS_DOT = (((1,), (0,)), ((), ()))


def halves(x):
    hi = x.astype(jnp.bfloat16)
    return hi, (x - hi.astype(jnp.float32)).astype(jnp.bfloat16)


def dot3(ah, al, bh, bl, dims):
    dot = functools.partial(
        lax.dot_general, dimension_numbers=dims, preferred_element_type=jnp.float32
    )
    return dot(ah, bh) + (dot(ah, bl) + dot(al, bh))


def kernel(cfg, weight, blocks, factors, ancestors, out, p_recv, f_full, fh, fl, s_full, s_hi, s_lo,
           upd, portion, xy_recv, zsum, z_recv, loc_sem, fs_sem, fr_sem, f2s_sem, f2r_sem, ps_sem, pr_sem,
           ss_sem, sr_sem, xs_sem, xr_sem, zs_sem, zr_sem, turn_sem):
    n, q_count, sups, nb, width, part, unit, split = cfg
    units = CORES * sups
    mid = units // 2
    rows_own = unit * part
    cols = width // units
    wide = lax.axis_index("wide")
    z = lax.axis_index("narrow")
    core = lax.rem(wide, CORES)
    q = lax.div(wide, CORES)
    mine = lax.rem(z, unit) * CORES + core
    my_unit = lax.div(z, unit)
    half = lax.div(my_unit, mid)
    far_sender = core != half

    def at(q_, core_, z_):
        return {"wide": q_ * CORES + core_, "narrow": z_}

    def order(i):
        h, j = i // mid, i % mid
        near = half * mid + lax.rem(my_unit - half * mid + j, mid)
        far = mid + j - half * (1 + 2 * j)
        return (1 - h) * near + h * far

    barrier = pltpu.get_barrier_semaphore()
    for i in range(1, CORES * n):
        other = lax.rem(z * CORES + core + i, CORES * n)
        pl.semaphore_signal(barrier, inc=1, device_id=at(q, lax.rem(other, CORES), lax.div(other, CORES)),
                            device_id_type=MESH)
    for i in range(1, q_count):
        pl.semaphore_signal(barrier, inc=1, device_id=at(lax.rem(q + i, q_count), core, z), device_id_type=MESH)
    pl.semaphore_wait(barrier, CORES * n - 1 + q_count - 1)

    anc_copy = pltpu.make_async_copy(ancestors.at[0], out.at[0], loc_sem)
    anc_copy.start()

    def remote(src, dst, send, recv, dev):
        return pltpu.make_async_remote_copy(src_ref=src, dst_ref=dst, send_sem=send, recv_sem=recv,
                                            device_id=dev, device_id_type=MESH)

    def source_copy(what, i, local):
        s, e = i // split, i % split
        chip = (core * sups + s) * unit + e // CORES
        rows = pl.ds(e * part, part)
        if what == "f":
            src, dst, ssem, rsem = factors.at[s, rows], f_full.at[z, e], fs_sem.at[i], fr_sem.at[z]
        else:
            src, dst, ssem, rsem = blocks.at[s, :, rows], p_recv.at[z], ps_sem.at[i], pr_sem.at[z]
        if local:
            return pltpu.make_async_copy(src, dst, rsem)
        return remote(src, dst, ssem, rsem, at(q, e % CORES, chip))

    def to_self(i):
        s, e = i // split, i % split
        return jnp.logical_and((core * sups + s) * unit + e // CORES == z, core == e % CORES)

    def send_all(what):
        for i in range(sups * split):
            @pl.when(to_self(i))
            def _():
                source_copy(what, i, True).start()

            @pl.when(jnp.logical_not(to_self(i)))
            def _():
                source_copy(what, i, False).start()

    inner = jnp.logical_or(my_unit == mid - 1, my_unit == mid)
    outer_unit = half * (units - 1)
    outer_far = jnp.logical_and(far_sender, my_unit == outer_unit)
    inner_far = jnp.logical_and(far_sender, inner)
    send_all("f")
    pl.when(jnp.logical_not(outer_far))(lambda: send_all("p"))

    def arrived(ref, sem):
        pltpu.make_async_copy(ref, ref, sem).wait()

    for i in range(n):
        arrived(f_full.at[i, mine], fr_sem.at[i])

    def peer(i):
        other = lax.rem(mine + i, split)
        return other, at(q, lax.rem(other, CORES), my_unit * unit + lax.div(other, CORES))

    f_copies = []
    for i in range(1, split):
        other, dev = peer(i)
        f_copies.append(remote(f_full.at[:, mine], f_full.at[:, mine], f2s_sem.at[other], f2r_sem.at[mine], dev))
        f_copies[-1].start()
    for i in range(1, split):
        other, dev = peer(i)
        arrived(f_full.at[:, other], f2r_sem.at[other])
    hi, lo = halves(f_full[...].reshape(width, width))
    fh[...] = hi
    fl[...] = lo

    def s_copy(zz, j):
        other, dev = peer(j)
        return remote(s_full.at[:, zz, mine], s_full.at[:, zz, mine], ss_sem.at[zz, other],
                      sr_sem.at[zz, mine], dev)

    def scale(a):
        for m in range(unit):
            zz = a * unit + m
            arrived(p_recv.at[zz], pr_sem.at[zz])
            ph, plo = halves(p_recv[zz].reshape(nb * part, width))
            s = dot3(ph, plo, fh[...], fl[...], COLS_DOT).reshape(nb, part, width)
            s_full[:, zz, mine] = s
            for j in range(1, split):
                s_copy(zz, j).start()
            sh, sl = halves(s)
            s_hi[:, zz, mine] = sh
            s_lo[:, zz, mine] = sl
        for m in range(unit):
            zz = a * unit + m
            for j in range(1, split):
                other, dev = peer(j)
                arrived(s_full.at[:, zz, other], sr_sem.at[zz, other])
                sh, sl = halves(s_full[:, zz, other])
                s_hi[:, zz, other] = sh
                s_lo[:, zz, other] = sl

    def xy_copy(a, b, other):
        return remote(portion.at[a, b, pl.ds(other * CORES, CORES)], xy_recv.at[q, a, b],
                      xs_sem.at[other, a, b], xr_sem.at[q, a, b], at(other, core, z))

    lefts = nb // 2

    def block(a, b):
        az, bz = pl.ds(a * unit, unit), pl.ds(b * unit, unit)
        for first in range(0, nb, lefts):
            ks, ls = pl.ds(first, nb - first), pl.ds(first, lefts)
            left = [r[ks, az, mine].reshape((nb - first) * rows_own, width) for r in (s_hi, s_lo)]
            right = [r[ls, bz].reshape(lefts * cols, width) for r in (s_hi, s_lo)]
            upd[first * rows_own:, first * cols:(first + lefts) * cols] = dot3(*left, *right, ROWS_DOT)

        def tiles(i, carry):
            other = lax.rem(q + 1 + i, q_count)
            sums = [None] * CORES
            p = 0
            for k in range(nb):
                for l in range(k + 1):
                    u = upd[k * rows_own:(k + 1) * rows_own, l * cols:(l + 1) * cols]
                    for c in range(CORES):
                        term = weight[other * CORES + c, p] * u
                        sums[c] = term if p == 0 else sums[c] + term
                    p += 1
            for c in range(CORES):
                portion[a, b, other * CORES + c] = sums[c]

            @pl.when(other != q)
            def _():
                xy_copy(a, b, other).start()

            return carry

        lax.fori_loop(0, q_count, tiles, 0)

    for i in range(units):
        if i == mid:
            @pl.when(inner_far)
            def _():
                for j in range(sups * split):
                    source_copy("p", j, False).wait_send()
                pl.semaphore_signal(turn_sem, inc=1, device_id=at(q, core, z - unit + 2 * unit * half),
                                    device_id_type=MESH)

            @pl.when(outer_far)
            def _():
                pl.semaphore_wait(turn_sem, 1)
                send_all("p")

        new = order(i)
        scale(new)

        def blocks_of(j, carry, i=i, new=new):
            old = jnp.minimum(j, i)
            row = order(old)
            block(row, order(jnp.where(j < i, i, j - i)))
            return carry

        lax.fori_loop(0, 2 * i + 1, blocks_of, 0)

    def z_copy(zz, c):
        return remote(zsum.at[zz, c], z_recv.at[z, core], zs_sem.at[zz, c], zr_sem.at[z, core], at(q, c, zz))

    def gather(i, carry):
        a = order(i)
        for b in range(units):
            total = portion[a, b, pl.ds(q * CORES, CORES)]
            for j in range(1, q_count):
                other = lax.rem(q + j, q_count)
                arrived(xy_recv.at[other, a, b], xr_sem.at[other, a, b])
                total = total + xy_recv[other, a, b]
            for m in range(unit):
                zsum[a * unit + m, :, :, b * cols:(b + 1) * cols] = total[:, m * part:(m + 1) * part]
        for m in range(unit):
            zz = a * unit + m
            for c in range(CORES):
                own = jnp.logical_and(zz == z, core == c)

                @pl.when(own)
                def _():
                    z_recv[z, core] = zsum[zz, c]

                @pl.when(jnp.logical_not(own))
                def _():
                    z_copy(zz, c).start()

        return carry

    lax.fori_loop(0, units, gather, 0)

    for i in range(1, CORES * n):
        other = lax.rem(z * CORES + core + i, CORES * n)
        oz, oc = lax.div(other, CORES), lax.rem(other, CORES)
        arrived(z_recv.at[oz, oc], zr_sem.at[oz, oc])
    anc_copy.wait()
    for e in range(split):
        rows = pl.ds(e * part, part)
        out[0, rows] = out[0, rows] - sum(z_recv[u * unit + e // CORES, e % CORES] for u in range(n // unit))

    for i in range(sups * split):
        @pl.when(jnp.logical_not(to_self(i)))
        def _():
            source_copy("f", i, False).wait_send()

        @pl.when(jnp.logical_not(jnp.logical_or(to_self(i), inner_far)))
        def _():
            source_copy("p", i, False).wait_send()
    for copy in f_copies:
        copy.wait_send()

    def sent(i, carry):
        for j in range(1, split):
            s_copy(i, j).wait_send()
        for c in range(CORES):
            @pl.when(jnp.logical_not(jnp.logical_and(i == z, core == c)))
            def _():
                z_copy(i, c).wait_send()
        return carry

    lax.fori_loop(0, n, sent, 0)

    def sent_xy(i, carry):
        for j in range(1, q_count):
            xy_copy(i // units, i % units, lax.rem(q + j, q_count)).wait_send()
        return carry

    lax.fori_loop(0, units * units, sent_xy, 0)


def shards(panels, factors, member, target, ancestors):
    sups, blk_count, nb = factors.shape[0], panels.shape[0], member.shape[1]
    width = panels.shape[2]
    n, wide_count = lax.axis_size("narrow"), lax.axis_size("wide")
    q_count = wide_count // CORES
    tile_count = ancestors.shape[0] * wide_count
    assert ancestors.shape[0] == 1 and n % (CORES * sups) == 0 and CORES == 2 and nb % 2 == 0 and sups == 2
    unit = n // (CORES * sups)
    split = unit * CORES
    part = panels.shape[1] // split
    wide, z = lax.axis_index("wide"), lax.axis_index("narrow")
    own_members = lax.dynamic_slice_in_dim(member, wide * sups, sups, 0) - wide * blk_count
    blocks = panels[own_members]
    supernode = (wide // CORES) * (CORES * sups) + z // unit
    own_targets = lax.dynamic_slice_in_dim(target, supernode, 1, 0)
    weight = (own_targets == jnp.arange(tile_count, dtype=jnp.int32)[:, None]).astype(jnp.float32)
    units = CORES * sups
    cols = width // units
    f32, bf16 = jnp.float32, jnp.bfloat16
    dma = pltpu.SemaphoreType.DMA
    cfg = (n, q_count, sups, nb, width, part, unit, split)
    any_space = pl.BlockSpec(memory_space=pl.ANY)
    return pl.pallas_call(
        functools.partial(kernel, cfg),
        out_shape=jax.ShapeDtypeStruct(ancestors.shape, f32),
        in_specs=[pl.BlockSpec(memory_space=pltpu.SMEM), any_space, any_space, any_space],
        out_specs=pl.BlockSpec(memory_space=pltpu.VMEM),
        scratch_shapes=[
            pltpu.VMEM((n, nb, part, width), f32),
            pltpu.VMEM((n, split, part, width), f32),
            pltpu.VMEM((width, width), bf16),
            pltpu.VMEM((width, width), bf16),
            pltpu.VMEM((nb, n, split, part, width), f32),
            pltpu.VMEM((nb, n, split, part, width), bf16),
            pltpu.VMEM((nb, n, split, part, width), bf16),
            pltpu.VMEM((nb * unit * part, nb * cols), f32),
            pltpu.VMEM((units, units, tile_count, unit * part, cols), f32),
            pltpu.VMEM((q_count, units, units, CORES, unit * part, cols), f32),
            pltpu.VMEM((n, CORES, part, width), f32),
            pltpu.VMEM((n, CORES, part, width), f32),
            dma,
            dma((sups * split,)), dma((n,)),
            dma((split,)), dma((split,)),
            dma((sups * split,)), dma((n,)),
            dma((n, split)), dma((n, split)),
            dma((q_count, units, units)), dma((q_count, units, units)),
            dma((n, CORES)), dma((n, CORES)),
            pltpu.SemaphoreType.REGULAR,
        ],
        compiler_params=pltpu.CompilerParams(
            collective_id=0, has_side_effects=True, vmem_limit_bytes=58 * 2**20
        ),
        name="level",
    )(weight, blocks, factors, ancestors)


def solution(mesh):
    return jax.shard_map(
        shards,
        mesh=mesh,
        in_specs=(
            P("wide", "narrow", None),
            P("wide", "narrow", None),
            P(),
            P(),
            P("wide", "narrow", None),
        ),
        out_specs=P("wide", "narrow", None),
        check_vma=False,
    )
```

profile of v0, /device:TPU:0, one launch (start us, length us, event | category | flops | bytes accessed | tf_op | source)
XLA Modules:
  0.0 105.1 jit_solution(11158928329794487560)
XLA Ops:
  0.0 0.0 copy-start
  0.0 0.8 dynamic-slice_bitcast_fusion
  0.8 0.8 compare_select_fusion
  1.6 0.1 copy.6
  1.7 0.1 reshape.2
  1.8 0.6 fusion.weight
  2.4 0.0 copy-done
  2.4 2.0 %gather_fusion = f32[8,128,512]{2,1,0:T(8,128)} fusion(f32[8,128,512]{2,1,0:T(8,128)S(1)} %copy-done, s32[1024]{0:T(1024)S(1)} %pad_clamp_fusion), kind=kCustom, calls=%fused_computation | custom fusion | bytes 4194336 | tf_op jit(solution)/shard_map/gather | solution.py:293
  4.4 99.0 %level.1 = f32[1,128,512]{2,1,0:T(8,128)} custom-call(f32[8,10]{1,0:T(8,128)} %fusion.weight, f32[2,4,128,512]{3,2,1,0:T(8,128)} %bitcast.3, f32[2,128,512]{2,1,0:T(8,128)} %factors.1, f32[1,128,512]{2,1,0:T(8,128)} %ancestors.1), custom_call_target="tpu_custom_call" | custom-call | tf_op jit(solution)/shard_map/level/pallas_call | solution.py:303
  103.4 1.7 %copy.8 = f32[1,128,512]{2,1,0:T(8,128)} copy(f32[1,128,512]{2,1,0:T(8,128)} %level.1) | data formatting | bytes 524288
  (1 shorter events, 0.0 us)
Async XLA Ops:
  0.0 2.4 %copy-start = (f32[8,128,512]{2,1,0:T(8,128)S(1)}, f32[8,128,512]{2,1,0:T(8,128)}, u32[]{:S(2)}) copy-start(f32[8,128,512]{2,1,0:T(8,128)} %param.5) | copy-start | bytes 6291460
where the time goes:
time: 106 us; the launch traced here: 105 us
  Pallas kernels  99 us (93%)
  local copies, waits for them, and re-layouts  4.72 us (4%)
  other arithmetic  1.36 us (1%)
    pallas_call x1, Pallas kernels, shards(): pl.pallas_call(functools.partial(kernel, cfg), out_shape=jax.ShapeDtypeSt...  99 us

commit v1 on v0

v1 whole, which is shorter than its diff:
```python
import functools

import jax
import jax.numpy as jnp
from jax import lax
from jax.experimental import pallas as pl
from jax.experimental.pallas import tpu as pltpu
from jax.sharding import PartitionSpec as P

MESH = pl.DeviceIdType.MESH
CORES = 2
PIECE = 32
SOURCES = 3
ROWS_DOT = (((1,), (1,)), ((), ()))
COLS_DOT = (((1,), (0,)), ((), ()))


def halves(x):
    hi = x.astype(jnp.bfloat16)
    return hi, (x - hi.astype(jnp.float32)).astype(jnp.bfloat16)


def dot3(ah, al, bh, bl, dims):
    dot = functools.partial(
        lax.dot_general, dimension_numbers=dims, preferred_element_type=jnp.float32
    )
    return dot(ah, bh) + (dot(ah, bl) + dot(al, bh))


def kernel(cfg, member, target, panels, factors, ancestors, out, pan, stage, p_recv, f_full, fh, fl,
           s_full, s_hi, s_lo, upd, portion, xy_recv, zsum, pair, z_recv, t_recv, turned,
           loc_sem, pan_sem, fs_sem, fr_sem, f2s_sem, f2r_sem, ps_sem, pr_sem, ss_sem, sr_sem,
           xs_sem, xr_sem, zs_sem, zr_sem, qs_sem, qr_sem, turn_sem):
    n, q_count, sups, nb, width, part, unit, split, pieces = cfg
    hr = part // pieces
    units = CORES * sups
    mid = units // 2
    last = units - 1
    cols = width // units
    rows_z = split * part
    wide = lax.axis_index("wide")
    z = lax.axis_index("narrow")
    core = lax.rem(wide, CORES)
    q = lax.div(wide, CORES)
    mine = lax.rem(z, unit) * CORES + core
    my_unit = lax.div(z, unit)
    half = lax.div(my_unit, mid)
    far_sender = core != half
    outer_unit = half * last
    far_outer = (1 - half) * last
    inner = my_unit != outer_unit
    supernode = q * units + my_unit

    def at(q_, core_, z_):
        return {"wide": q_ * CORES + core_, "narrow": z_}

    def order(i):
        h, j = i // mid, i % mid
        near = half * mid + lax.rem(my_unit - half * mid + j, mid)
        far = mid + j - half * (1 + 2 * j)
        return (1 - h) * near + h * far

    def remote(src, dst, send, recv, dev):
        return pltpu.make_async_remote_copy(src_ref=src, dst_ref=dst, send_sem=send, recv_sem=recv,
                                            device_id=dev, device_id_type=MESH)

    def arrived(ref, sem):
        pltpu.make_async_copy(ref, ref, sem).wait()

    def piece(h):
        return pl.ds(h * hr if isinstance(h, int) else pl.multiple_of(h * hr, hr), hr)

    pan_copy = pltpu.make_async_copy(panels, pan, pan_sem)
    pan_copy.start()
    anc_copy = pltpu.make_async_copy(ancestors.at[0], out.at[0], loc_sem)
    anc_copy.start()

    barrier = pltpu.get_barrier_semaphore()
    for i in range(1, CORES * n):
        other = lax.rem(z * CORES + core + i, CORES * n)
        pl.semaphore_signal(barrier, inc=1, device_id=at(q, lax.rem(other, CORES), lax.div(other, CORES)),
                            device_id_type=MESH)
    for i in range(1, q_count):
        pl.semaphore_signal(barrier, inc=1, device_id=at(lax.rem(q + i, q_count), core, z), device_id_type=MESH)
    pl.semaphore_wait(barrier, CORES * n - 1 + q_count - 1)

    def chip_of(s, e):
        return (core * sups + s) * unit + e // CORES

    def to_self(s, e):
        return jnp.logical_and(chip_of(s, e) == z, core == e % CORES)

    def f_source(s, e, local):
        src, dst = factors.at[s, pl.ds(e * part, part)], f_full.at[z, e]
        if local:
            return pltpu.make_async_copy(src, dst, fr_sem.at[z])
        return remote(src, dst, fs_sem.at[s, e], fr_sem.at[z], at(q, e % CORES, chip_of(s, e)))

    def nearest(i):
        return lax.rem(i + 1 - core, sups)

    def p_source(s, e, h):
        src = stage.at[s, :, pl.ds(e * part + h * hr, hr)]
        return remote(src, p_recv.at[z, h], ps_sem.at[s, e, h], pr_sem.at[z, h], at(q, e % CORES, chip_of(s, e)))

    parts = [(i, e) for i in range(sups) for e in range(split)]
    for i, e in parts:
        s = nearest(i)

        @pl.when(to_self(s, e))
        def _():
            f_source(s, e, True).start()

        @pl.when(jnp.logical_not(to_self(s, e)))
        def _():
            f_source(s, e, False).start()

    pan_copy.wait()

    def pick(i, carry):
        s, k = lax.div(i, nb), lax.rem(i, nb)
        stage[s, k] = pan[lax.rem(member[wide * sups + s, k], sups * nb)]
        return carry

    lax.fori_loop(0, sups * nb, pick, 0)

    far_inner = jnp.logical_and(far_sender, inner)
    far_outer_sender = jnp.logical_and(far_sender, jnp.logical_not(inner))
    p_list = [(i, e, h) for h in range(pieces) for i, e in parts]

    def send_panels():
        for i, e, h in p_list:
            s = nearest(i)

            @pl.when(to_self(s, e))
            def _():
                p_recv[z, h] = stage[s, :, pl.ds(e * part + h * hr, hr)]

            @pl.when(jnp.logical_not(to_self(s, e)))
            def _():
                p_source(s, e, h).start()

    pl.when(jnp.logical_not(far_outer_sender))(send_panels)

    for i in range(n):
        arrived(f_full.at[i, mine], fr_sem.at[i])

    def peer(i):
        other = lax.rem(mine + i, split)
        return other, at(q, lax.rem(other, CORES), my_unit * unit + lax.div(other, CORES))

    f_copies = []
    for i in range(1, split):
        other, dev = peer(i)
        f_copies.append(remote(f_full.at[:, mine], f_full.at[:, mine], f2s_sem.at[other], f2r_sem.at[mine], dev))
        f_copies[-1].start()
    for i in range(1, split):
        other, dev = peer(i)
        arrived(f_full.at[:, other], f2r_sem.at[other])
    hi, lo = halves(f_full[...].reshape(width, width))
    fh[...] = hi
    fl[...] = lo

    def s_copy(zz, h, j):
        other, dev = peer(j)
        ref = s_full.at[:, zz, mine, piece(h)]
        return remote(ref, ref, ss_sem.at[zz, h, other], sr_sem.at[zz, h, mine], dev)

    def scale(zz, h):
        @pl.when(jnp.logical_not(jnp.logical_and(zz == z, core == half)))
        def _():
            arrived(p_recv.at[zz, h], pr_sem.at[zz, h])

        ph, plo = halves(p_recv[zz, h].reshape(nb * hr, width))
        s = dot3(ph, plo, fh[...], fl[...], COLS_DOT).reshape(nb, hr, width)
        s_full[:, zz, mine, piece(h)] = s
        for j in range(1, split):
            s_copy(zz, h, j).start()
        s_hi[:, zz, mine, piece(h)], s_lo[:, zz, mine, piece(h)] = halves(s)

    def take(zz, h):
        for j in range(1, split):
            other, dev = peer(j)
            arrived(s_full.at[:, zz, other, piece(h)], sr_sem.at[zz, h, other])
            s_hi[:, zz, other, piece(h)], s_lo[:, zz, other, piece(h)] = halves(s_full[:, zz, other, piece(h)])

    def scale_all(a):
        def one(i, carry):
            scale(a * unit + lax.div(i, pieces), lax.rem(i, pieces))
            return carry

        def two(i, carry):
            take(a * unit + lax.div(i, pieces), lax.rem(i, pieces))
            return carry

        lax.fori_loop(0, unit * pieces, one, 0)
        lax.fori_loop(0, unit * pieces, two, 0)

    def xy_copy(r, c, h, other):
        return remote(portion.at[r, c, h, pl.ds(other * CORES, CORES)], xy_recv.at[q, r, c, h],
                      xs_sem.at[other, r, c, h], xr_sem.at[q, r, c, h], at(other, core, z))

    two = nb // 2

    def block(a, b, h=None, flip=False):
        rows = unit * (part if h is None else hr)
        bz, az = pl.ds(b * unit, unit), pl.ds(a * unit, unit)
        for first in range(0, nb, two):
            lo_k, hi_k = (0, first + two) if flip else (first, nb)
            ks, ls = pl.ds(lo_k, hi_k - lo_k), pl.ds(first, two)
            left = [(r[ks, az, mine] if h is None else r[ks, az, mine, piece(h)]).reshape((hi_k - lo_k) * rows, width)
                    for r in (s_hi, s_lo)]
            right = [r[ls, bz].reshape(two * cols, width) for r in (s_hi, s_lo)]
            upd[lo_k * rows:hi_k * rows, first * cols:(first + two) * cols] = dot3(*left, *right, ROWS_DOT)
        r, c = (b, a) if flip else (a, b)

        def tiles(i, carry):
            other = lax.rem(q + 1 + i, q_count)
            sums = [None] * CORES
            p = 0
            for k in range(nb):
                for l in range(k + 1):
                    x, y = (l, k) if flip else (k, l)
                    u = upd[x * rows:(x + 1) * rows, y * cols:(y + 1) * cols]
                    for t in range(CORES):
                        term = (target[supernode, p] == other * CORES + t).astype(jnp.float32) * u
                        sums[t] = term if p == 0 else sums[t] + term
                    p += 1
            hs = range(pieces) if h is None else (h,)
            for t in range(CORES):
                for m in range(unit):
                    for g, hh in enumerate(hs):
                        first = (m * len(hs) + g) * hr
                        portion[r, c, hh, other * CORES + t, m] = sums[t][first:first + hr]

            @pl.when(other != q)
            def _():
                for hh in hs:
                    xy_copy(r, c, hh, other).start()

            return carry

        lax.fori_loop(0, q_count, tiles, 0)

    def item(i, j):
        new_row = j <= i
        return (order(jnp.where(new_row, i, j - i - 1)), order(jnp.where(new_row, j, i)))

    def step(i):
        scale_all(order(i))

        def one(j, carry):
            block(*item(i, j))
            return carry

        lax.fori_loop(0, 2 * i + 1, one, 0)

    def last_item(j):
        newest = j < last
        other = order(lax.rem(j, last))
        return jnp.where(newest, far_outer, other), jnp.where(newest, other, far_outer)

    def last_step(h):
        for m in range(unit):
            scale(far_outer * unit + m, h)
        for m in range(unit):
            take(far_outer * unit + m, h)

        def one(j, carry):
            block(far_outer, order(j), h)
            return carry

        def flipped(j, carry):
            block(far_outer, order(j), h, True)
            return carry

        lax.fori_loop(0, last, one, 0)
        lax.fori_loop(0, last, flipped, 0)

    def is_near(r):
        return lax.div(r, mid) == half

    def deliver(r, c, h, what):
        near = is_near(r)
        src = jnp.where(near, jnp.where(r == my_unit, 0, 1), SOURCES - 1)
        flip = jnp.logical_and(c == far_outer, r != far_outer)
        for t in range(CORES):
            for m in range(unit):
                zz = r * unit + m
                own = jnp.logical_and(zz == z, core == t)
                send, recv, dev = zs_sem.at[r, c, h, t, m], zr_sem.at[src, c, mine, h], at(q, t, zz)
                plain = remote(zsum.at[r, c, h, t, m], z_recv.at[src, c, mine, h], send, recv, dev)
                flipped = remote(zsum.at[r, c, h, t], t_recv.at[src, :, mine, h], send, recv, dev)

                if what == "start":
                    @pl.when(jnp.logical_and(own, jnp.logical_not(flip)))
                    def _():
                        z_recv[0, c, mine, h] = zsum[r, c, h, t, m]

                    @pl.when(jnp.logical_and(own, flip))
                    def _():
                        t_recv[0, :, mine, h] = zsum[r, c, h, t]

                @pl.when(jnp.logical_and(jnp.logical_not(own), jnp.logical_not(flip)))
                def _():
                    plain.start() if what == "start" else plain.wait_send()

                @pl.when(jnp.logical_and(jnp.logical_not(own), flip))
                def _():
                    flipped.start() if what == "start" else flipped.wait_send()

    def pair_copy(r, c, h):
        f = lax.rem(r, mid)
        dev = at(q, core, z + unit - 2 * unit * half)
        return remote(zsum.at[r, c, h], pair.at[f, c, h], qs_sem.at[f, c, h], qr_sem.at[f, c, h], dev)

    def gather(r, c, h):
        total = portion[r, c, h, pl.ds(q * CORES, CORES)]
        for j in range(1, q_count):
            other = lax.rem(q + j, q_count)
            arrived(xy_recv.at[other, r, c, h], xr_sem.at[other, r, c, h])
            total = total + xy_recv[other, r, c, h]
        zsum[r, c, h] = total

        @pl.when(is_near(r))
        def _():
            deliver(r, c, h, "start")

        @pl.when(jnp.logical_not(jnp.logical_or(is_near(r), inner)))
        def _():
            pair_copy(r, c, h).start()

    def join(r, c, h):
        @pl.when(jnp.logical_and(inner, jnp.logical_not(is_near(r))))
        def _():
            f = lax.rem(r, mid)
            arrived(pair.at[f, c, h], qr_sem.at[f, c, h])
            zsum[r, c, h] = zsum[r, c, h] + pair[f, c, h]
            deliver(r, c, h, "start")

    def over(do, i):
        def one(j, carry):
            do(*item(i, lax.div(j, pieces)), lax.rem(j, pieces))
            return carry

        lax.fori_loop(0, (2 * i + 1) * pieces, one, 0)

    def over_last(do, h):
        def one(j, carry):
            do(*last_item(j), h)
            return carry

        lax.fori_loop(0, 2 * last, one, 0)

    def over_corner(do):
        def one(h, carry):
            do(far_outer, far_outer, h)
            return carry

        lax.fori_loop(0, pieces, one, 0)

    step(0)
    step(1)

    @pl.when(far_inner)
    def _():
        for i, e, h in p_list[:-1]:
            p_source(nearest(i), e, h).wait_send()
        pl.semaphore_signal(turn_sem, inc=1, device_id=at(q, core, z - unit + 2 * unit * half),
                            device_id_type=MESH)

    @pl.when(far_outer_sender)
    def _():
        pl.semaphore_wait(turn_sem, 1)
        send_panels()

    step(2)
    over(gather, 0)
    over(gather, 1)
    for h in range(pieces):
        last_step(h)
        if h == 0:
            over(gather, 2)
    block(far_outer, far_outer)
    over(join, 2)
    for h in range(pieces):
        over_last(gather, h)
        over_last(join, h)
    over_corner(gather)
    over_corner(join)

    anc_copy.wait()
    row0 = pl.multiple_of(lax.rem(z, unit) * rows_z, rows_z)
    for src in range(SOURCES):
        outermost = far_outer if src < SOURCES - 1 else outer_unit
        for c in range(units):
            flip = outermost == c
            if src == SOURCES - 1:
                flip = jnp.logical_and(flip, inner)

            def wait(flipped):
                for e in range(split):
                    for h in range(pieces):
                        def one():
                            arrived(t_recv.at[src, :, e, h] if flipped else z_recv.at[src, c, e, h],
                                    zr_sem.at[src, c, e, h])

                        one() if src else pl.when(mine != e)(one)

            @pl.when(flip)
            def _():
                wait(True)
                turned[...] = t_recv[src].reshape(cols, cols).T
                out[0, :, c * cols:(c + 1) * cols] = (
                    out[0, :, c * cols:(c + 1) * cols] - turned[pl.ds(row0, rows_z)])

            @pl.when(jnp.logical_not(flip))
            def _():
                wait(False)
                out[0, :, c * cols:(c + 1) * cols] = (
                    out[0, :, c * cols:(c + 1) * cols] - z_recv[src, c].reshape(rows_z, cols))

    for i, e in parts:
        s = nearest(i)

        @pl.when(jnp.logical_not(to_self(s, e)))
        def _():
            f_source(s, e, False).wait_send()

    for i, e, h in p_list[:-1]:
        s = nearest(i)

        @pl.when(jnp.logical_not(jnp.logical_or(to_self(s, e), far_inner)))
        def _():
            p_source(s, e, h).wait_send()

    i, e, h = p_list[-1]

    @pl.when(jnp.logical_not(to_self(nearest(i), e)))
    def _():
        p_source(nearest(i), e, h).wait_send()

    for copy in f_copies:
        copy.wait_send()

    def sent(i, carry):
        for j in range(1, split):
            s_copy(lax.div(i, pieces), lax.rem(i, pieces), j).wait_send()
        return carry

    lax.fori_loop(0, n * pieces, sent, 0)

    def sent_sums(i, carry):
        h, c, r = lax.rem(i, pieces), lax.rem(lax.div(i, pieces), units), lax.div(i, pieces * units)
        for j in range(1, q_count):
            xy_copy(r, c, h, lax.rem(q + j, q_count)).wait_send()

        @pl.when(jnp.logical_or(is_near(r), inner))
        def _():
            deliver(r, c, h, "wait")

        @pl.when(jnp.logical_not(jnp.logical_or(is_near(r), inner)))
        def _():
            pair_copy(r, c, h).wait_send()

        return carry

    lax.fori_loop(0, units * units * pieces, sent_sums, 0)


def shards(panels, factors, member, target, ancestors):
    sups, blk_count, nb = factors.shape[0], panels.shape[0], member.shape[1]
    width = panels.shape[2]
    n, wide_count = lax.axis_size("narrow"), lax.axis_size("wide")
    q_count = wide_count // CORES
    tile_count = ancestors.shape[0] * wide_count
    assert ancestors.shape[0] == 1 and n % (CORES * sups) == 0 and nb % 2 == 0 and sups == 2
    assert blk_count == sups * nb
    unit = n // (CORES * sups)
    split = unit * CORES
    part = panels.shape[1] // split
    pieces = max(1, part // PIECE)
    hr = part // pieces
    units = CORES * sups
    cols = width // units
    f32, bf16 = jnp.float32, jnp.bfloat16
    dma = pltpu.SemaphoreType.DMA
    cfg = (n, q_count, sups, nb, width, part, unit, split, pieces)
    any_space = pl.BlockSpec(memory_space=pl.ANY)
    smem = pl.BlockSpec(memory_space=pltpu.SMEM)
    return pl.pallas_call(
        functools.partial(kernel, cfg),
        out_shape=jax.ShapeDtypeStruct(ancestors.shape, f32),
        in_specs=[smem, smem, any_space, any_space, any_space],
        out_specs=pl.BlockSpec(memory_space=pltpu.VMEM),
        scratch_shapes=[
            pltpu.VMEM(panels.shape, f32),
            pltpu.VMEM((sups, nb, panels.shape[1], width), f32),
            pltpu.VMEM((n, pieces, nb, hr, width), f32),
            pltpu.VMEM((n, split, part, width), f32),
            pltpu.VMEM((width, width), bf16),
            pltpu.VMEM((width, width), bf16),
            pltpu.VMEM((nb, n, split, part, width), f32),
            pltpu.VMEM((nb, n, split, part, width), bf16),
            pltpu.VMEM((nb, n, split, part, width), bf16),
            pltpu.VMEM((nb * unit * part, nb * cols), f32),
            pltpu.VMEM((units, units, pieces, tile_count, unit, hr, cols), f32),
            pltpu.VMEM((q_count, units, units, pieces, CORES, unit, hr, cols), f32),
            pltpu.VMEM((units, units, pieces, CORES, unit, hr, cols), f32),
            pltpu.VMEM((units // 2, units, pieces, CORES, unit, hr, cols), f32),
            pltpu.VMEM((SOURCES, units, split, pieces, hr, cols), f32),
            pltpu.VMEM((SOURCES, unit, split, pieces, hr, cols), f32),
            pltpu.VMEM((cols, cols), f32),
            dma, dma,
            dma((sups, split)), dma((n,)),
            dma((split,)), dma((split,)),
            dma((sups, split, pieces)), dma((n, pieces)),
            dma((n, pieces, split)), dma((n, pieces, split)),
            dma((q_count, units, units, pieces)), dma((q_count, units, units, pieces)),
            dma((units, units, pieces, CORES, unit)), dma((SOURCES, units, split, pieces)),
            dma((units // 2, units, pieces)), dma((units // 2, units, pieces)),
            pltpu.SemaphoreType.REGULAR,
        ],
        compiler_params=pltpu.CompilerParams(
            collective_id=0, has_side_effects=True, vmem_limit_bytes=58 * 2**20
        ),
        name="level",
    )(member, target, panels, factors, ancestors)


def solution(mesh):
    return jax.shard_map(
        shards,
        mesh=mesh,
        in_specs=(
            P("wide", "narrow", None),
            P("wide", "narrow", None),
            P(),
            P(),
            P("wide", "narrow", None),
        ),
        out_specs=P("wide", "narrow", None),
        check_vma=False,
    )
```

time: 106 us -> 118 us (1.11)
  Pallas kernels: 99 us -> 115 us
  local copies, waits for them, and re-layouts: 4.72 us -> 3.03 us
  other arithmetic: 1.36 us -> 0 us
    pallas_call x1, Pallas kernels: 99 us -> 115 us  [shards(): pl.pallas_call(functools.partial(kernel, cfg), out_shape=jax.ShapeDtypeSt...]
    gather x1 -> x0, local copies, waits for them, and re-layouts: 2.03 us -> none  [shards(): blocks = panels[own_members]]
    unnamed x3 -> x2, local copies, waits for them, and re-layouts: 1.68 us -> 3.03 us
where the time goes in v1:
time: 118 us
  Pallas kernels  115 us (97%)
  local copies, waits for them, and re-layouts  3.03 us (3%)
    pallas_call x1, Pallas kernels, shards(): pl.pallas_call(functools.partial(kernel, cfg), out_shape=jax.ShapeDtypeSt...  115 us
    unnamed x2, local copies, waits for them, and re-layouts  3.03 us

profile of v1, /device:TPU:0, one launch (start us, length us, event | category | flops | bytes accessed | tf_op | source)
XLA Modules:
  0.0 117.6 jit_solution(9389588331265480354)
XLA Ops:
  0.0 1.4 %copy.6.member = s32[16,4]{1,0:T(8,128)} copy(s32[16,4]{0,1:T(4,128)} %param.7) | data formatting | bytes 512 | tf_op args[2]
  1.4 114.6 %level.1 = f32[1,128,512]{2,1,0:T(8,128)} custom-call(s32[16,4]{1,0:T(8,128)} %copy.6.member, s32[16,10]{1,0:T(8,128)} %target.1, f32[8,128,512]{2,1,0:T(8,128)} %panels.1, f32[2,128,512]{2,1,0:T(8,128)} %factors.1, f32[1,128,512]{2,1,0:T(8,128)} %ancestors.1), custom_call_target="tpu_custom_call" | custom-call | tf_op jit(solution)/shard_map/level/pallas_call | solution.py:491
  116.0 1.7 %copy.8 = f32[1,128,512]{2,1,0:T(8,128)} copy(f32[1,128,512]{2,1,0:T(8,128)} %level.1) | data formatting | bytes 524288

commit v2 on v1

v2 whole, which is shorter than its diff:
```python
import functools
import math

import jax
import jax.numpy as jnp
from jax import lax
from jax.experimental import pallas as pl
from jax.experimental.pallas import tpu as pltpu
from jax.sharding import PartitionSpec as P

MESH = pl.DeviceIdType.MESH
CORES = 2
PIECE = 32
SOURCES = 3
ROWS_DOT = (((1,), (1,)), ((), ()))
COLS_DOT = (((1,), (0,)), ((), ()))


def halves(x):
    hi = x.astype(jnp.bfloat16)
    return hi, (x - hi.astype(jnp.float32)).astype(jnp.bfloat16)


def dot3(ah, al, bh, bl, dims):
    dot = functools.partial(
        lax.dot_general, dimension_numbers=dims, preferred_element_type=jnp.float32
    )
    return dot(ah, bh) + (dot(ah, bl) + dot(al, bh))


def kernel(cfg, member, target, panels, factors, ancestors, out, pan, stage, p_recv, f_full, fh, fl,
           s_full, s_hi, s_lo, upd, portion, recv1, recv2, zsum, pair, z_recv, t_recv, turned, relay,
           loc_sem, pan_sem, fs_sem, fr_sem, f2s_sem, f2r_sem, ps_sem, pr_sem, ss_sem, sr_sem,
           xs1_sem, xr1_sem, xs2_sem, xr2_sem, zs_sem, zr_sem, qs_sem, qr_sem, rr_sem, rf_sem):
    n, side, sups, nb, width, part, unit, split, pieces = cfg
    hr = part // pieces
    units = CORES * sups
    mid = units // 2
    last = units - 1
    cols = width // units
    rows_z = split * part
    wide = lax.axis_index("wide")
    z = lax.axis_index("narrow")
    core = lax.rem(wide, CORES)
    q = lax.div(wide, CORES)
    mine = lax.rem(z, unit) * CORES + core
    my_unit = lax.div(z, unit)
    half = lax.div(my_unit, mid)
    far_sender = core != half
    outer_unit = half * last
    far_outer = (1 - half) * last
    inner = my_unit != outer_unit
    supernode = q * units + my_unit
    row, col = lax.div(q, side), lax.rem(q, side)

    def at(q_, core_, z_):
        return {"wide": q_ * CORES + core_, "narrow": z_}

    def order(i):
        h, j = i // mid, i % mid
        near = half * mid + lax.rem(my_unit - half * mid + j, mid)
        far = mid + j - half * (1 + 2 * j)
        return (1 - h) * near + h * far

    def remote(src, dst, send, recv, dev):
        return pltpu.make_async_remote_copy(src_ref=src, dst_ref=dst, send_sem=send, recv_sem=recv,
                                            device_id=dev, device_id_type=MESH)

    def arrived(ref, sem):
        pltpu.make_async_copy(ref, ref, sem).wait()

    def piece(h):
        return pl.ds(h * hr if isinstance(h, int) else pl.multiple_of(h * hr, hr), hr)

    pan_copy = pltpu.make_async_copy(panels, pan, pan_sem)
    pan_copy.start()
    anc_copy = pltpu.make_async_copy(ancestors.at[0], out.at[0], loc_sem)
    anc_copy.start()

    barrier = pltpu.get_barrier_semaphore()
    for i in range(1, CORES * n):
        other = lax.rem(z * CORES + core + i, CORES * n)
        pl.semaphore_signal(barrier, inc=1, device_id=at(q, lax.rem(other, CORES), lax.div(other, CORES)),
                            device_id_type=MESH)
    for i in range(1, side):
        for other in (row * side + lax.rem(col + i, side), lax.rem(row + i, side) * side + col):
            pl.semaphore_signal(barrier, inc=1, device_id=at(other, core, z), device_id_type=MESH)
    pl.semaphore_wait(barrier, CORES * n - 1 + 2 * (side - 1))

    def chip_of(s, e):
        return (core * sups + s) * unit + e // CORES

    def to_self(s, e):
        return jnp.logical_and(chip_of(s, e) == z, core == e % CORES)

    def f_source(s, e, local):
        src, dst = factors.at[s, pl.ds(e * part, part)], f_full.at[z, e]
        if local:
            return pltpu.make_async_copy(src, dst, fr_sem)
        return remote(src, dst, fs_sem, fr_sem, at(q, e % CORES, chip_of(s, e)))

    def nearest(i):
        return lax.rem(i + 1 - core, sups)

    def p_source(s, e, h):
        src = stage.at[s, :, pl.ds(e * part + h * hr, hr)]
        return remote(src, p_recv.at[z, h], ps_sem, pr_sem.at[z, h], at(q, e % CORES, chip_of(s, e)))

    parts = [(i, e) for i in range(sups) for e in range(split)]
    for i, e in parts:
        s = nearest(sups - 1 - i)

        @pl.when(to_self(s, e))
        def _():
            f_source(s, e, True).start()

        @pl.when(jnp.logical_not(to_self(s, e)))
        def _():
            f_source(s, e, False).start()

    pan_copy.wait()

    def pick(i, carry):
        s, k = lax.div(i, nb), lax.rem(i, nb)
        stage[s, k] = pan[lax.rem(member[wide * sups + s, k], sups * nb)]
        return carry

    lax.fori_loop(0, sups * nb, pick, 0)

    far_inner = jnp.logical_and(far_sender, inner)
    far_outer_sender = jnp.logical_and(far_sender, jnp.logical_not(inner))
    p_list = [(i, e, h) for i in range(sups) for h in range(pieces) for e in range(split)]
    relay_list = [(i, e, h) for h in range(pieces) for i in reversed(range(sups)) for e in range(split)]
    ahead = relay_list[:sups * split * max(1, pieces // 2)]

    def slot(s, e, h):
        return (s * split + e) * pieces + h

    def to_relay(i, e, h):
        s = nearest(i)
        src = stage.at[s, :, pl.ds(e * part + h * hr, hr)]
        return remote(src, relay.at[slot(s, e, h)], ps_sem, rr_sem.at[slot(s, e, h)],
                      at(q, core, z + unit - 2 * unit * half))

    def from_relay(i, e, h):
        s, outer_z = nearest(i), z - unit + 2 * unit * half
        return remote(relay.at[slot(s, e, h)], p_recv.at[outer_z, h], rf_sem, pr_sem.at[outer_z, h],
                      at(q, e % CORES, chip_of(s, e)))

    def send_relay():
        for which in relay_list:
            to_relay(*which).start()

    def pass_on(some):
        for i, e, h in some:
            which = slot(nearest(i), e, h)
            arrived(relay.at[which], rr_sem.at[which])
            from_relay(i, e, h).start()

    def send_panels():
        for i, e, h in p_list:
            s = nearest(i)

            @pl.when(to_self(s, e))
            def _():
                p_recv[z, h] = stage[s, :, pl.ds(e * part + h * hr, hr)]

            @pl.when(jnp.logical_not(to_self(s, e)))
            def _():
                p_source(s, e, h).start()

    pl.when(jnp.logical_not(far_outer_sender))(send_panels)

    arrived(f_full.at[:, mine], fr_sem)

    def peer(i):
        other = lax.rem(mine + i, split)
        return other, at(q, lax.rem(other, CORES), my_unit * unit + lax.div(other, CORES))

    f_copies = []
    for i in range(1, split):
        other, dev = peer(i)
        f_copies.append(remote(f_full.at[:, mine], f_full.at[:, mine], f2s_sem, f2r_sem, dev))
        f_copies[-1].start()
    others = pl.ds(0, split - 1)
    arrived(f_full.at[:, others], f2r_sem)
    hi, lo = halves(f_full[...].reshape(width, width))
    fh[...] = hi
    fl[...] = lo

    def s_copy(zz, h, j):
        other, dev = peer(j)
        ref = s_full.at[:, zz, mine, piece(h)]
        return remote(ref, ref, ss_sem, sr_sem.at[zz, h], dev)

    def scale(zz, h):
        @pl.when(jnp.logical_not(jnp.logical_and(zz == z, core == half)))
        def _():
            arrived(p_recv.at[zz, h], pr_sem.at[zz, h])

        ph, plo = halves(p_recv[zz, h].reshape(nb * hr, width))
        s = dot3(ph, plo, fh[...], fl[...], COLS_DOT).reshape(nb, hr, width)
        s_full[:, zz, mine, piece(h)] = s
        for j in range(1, split):
            s_copy(zz, h, j).start()
        s_hi[:, zz, mine, piece(h)], s_lo[:, zz, mine, piece(h)] = halves(s)

    def take(zz, h):
        arrived(s_full.at[:, zz, others, piece(h)], sr_sem.at[zz, h])
        for j in range(1, split):
            other, _ = peer(j)
            s_hi[:, zz, other, piece(h)], s_lo[:, zz, other, piece(h)] = halves(s_full[:, zz, other, piece(h)])

    def scale_all(a, between=None):
        def one(i, carry):
            scale(a * unit + lax.div(i, pieces), lax.rem(i, pieces))
            return carry

        def two(i, carry):
            take(a * unit + lax.div(i, pieces), lax.rem(i, pieces))
            return carry

        lax.fori_loop(0, unit * pieces, one, 0)
        if between is not None:
            between()
        lax.fori_loop(0, unit * pieces, two, 0)

    def place(r, c, h):
        along_row = jnp.logical_or(r > c, jnp.logical_and(r == c, h == 0))
        return along_row, jnp.where(along_row, col, row), jnp.where(along_row, row, col)

    def q_at(along_row, f, g):
        return jnp.where(along_row, g * side + f, f * side + g)

    def steps(src, dst):
        return lax.rem(src - dst - 1 + side, side)

    def mark(r, c, h):
        in_pieces = jnp.logical_and(r != c, jnp.logical_or(r == far_outer, c == far_outer))
        other = r + c - far_outer
        return (jnp.where(in_pieces, jnp.where(h == 0, far_outer, other), r),
                jnp.where(in_pieces, jnp.where(h == 0, other, far_outer), c))

    def first_copy(r, c, h, f):
        along_row, mine_f, mine_g = place(r, c, h)
        d = steps(mine_f, f)
        return remote(portion.at[r, c, h, pl.ds(f * side * CORES, side * CORES)], recv1.at[r, c, h, d],
                      xs1_sem, xr1_sem.at[*mark(r, c, h), d], at(q_at(along_row, f, mine_g), core, z))

    def second_copy(r, c, h, g):
        along_row, mine_f, mine_g = place(r, c, h)
        d = steps(mine_g, g)
        return remote(portion.at[r, c, h, pl.ds((mine_f * side + g) * CORES, CORES)], recv2.at[r, c, h, d],
                      xs2_sem, xr2_sem.at[*mark(r, c, h), d], at(q_at(along_row, mine_f, g), core, z))

    two = nb // 2

    def products(a, b, h=None):
        rows = unit * (part if h is None else hr)
        bz, az = pl.ds(b * unit, unit), pl.ds(a * unit, unit)
        for first in range(0, nb, two):
            low = first if h is None else 0
            ks, ls = pl.ds(low, nb - low), pl.ds(first, two)
            left = [(r[ks, az, mine] if h is None else r[ks, az, mine, piece(h)]).reshape((nb - low) * rows, width)
                    for r in (s_hi, s_lo)]
            right = [r[ls, bz].reshape(two * cols, width) for r in (s_hi, s_lo)]
            upd[low * rows:nb * rows, first * cols:(first + two) * cols] = dot3(*left, *right, ROWS_DOT)

    def sums_of(r, c, h=None, flip=False):
        hs = range(pieces) if h is None else (h,)
        rows = unit * len(hs) * hr

        def tiles(i, carry):
            i = lax.rem(q + 1 + i, side * side)
            oq, og = lax.div(i, side), lax.rem(i, side)
            sums = [None] * CORES
            p = 0
            for k in range(nb):
                for l in range(k + 1):
                    x, y = (l, k) if flip else (k, l)
                    u = upd[x * rows:(x + 1) * rows, y * cols:(y + 1) * cols]
                    for t in range(CORES):
                        term = (target[supernode, p] == i * CORES + t).astype(jnp.float32) * u
                        sums[t] = term if p == 0 else sums[t] + term
                    p += 1
            for x, hh in enumerate(hs):
                along_row, mine_f, mine_g = place(r, c, hh)
                f, g = jnp.where(along_row, og, oq), jnp.where(along_row, oq, og)
                for t in range(CORES):
                    for m in range(unit):
                        first = (m * len(hs) + x) * hr
                        portion[r, c, hh, (f * side + g) * CORES + t, m] = sums[t][first:first + hr]
            return carry

        lax.fori_loop(0, side * side, tiles, 0)
        for hh in hs:
            _, mine_f, _ = place(r, c, hh)
            for j in range(1, side):
                first_copy(r, c, hh, lax.rem(mine_f + j, side)).start()

    def block(a, b):
        products(a, b)
        sums_of(a, b)

    def item(i, j):
        new_row = j <= i
        return (order(jnp.where(new_row, i, j - i - 1)), order(jnp.where(new_row, j, i)))

    def step(i):
        scale_all(order(i), (lambda: pl.when(far_outer_sender)(send_relay)) if i == 1 else None)

        def one(j, carry):
            block(*item(i, j))
            return carry

        lax.fori_loop(0, 2 * i + 1, one, 0)

    def last_step(h, between=None):
        for m in range(unit):
            scale(far_outer * unit + m, h)
        if between is not None:
            between()
        for m in range(unit):
            take(far_outer * unit + m, h)

        def one(j, carry):
            products(far_outer, order(j), h)
            sums_of(far_outer, order(j), h)
            sums_of(order(j), far_outer, h, True)
            return carry

        lax.fori_loop(0, last, one, 0)

    def is_near(r):
        return lax.div(r, mid) == half

    def total_at(r, c, h, t=0, m=0):
        return (((r * units + c) * pieces + h) * CORES + t) * unit + m

    def deliver(r, c, h):
        near = is_near(r)
        src = jnp.where(near, jnp.where(r == my_unit, 0, 1), SOURCES - 1)
        flip = jnp.logical_and(c == far_outer, r != far_outer)
        for t in range(CORES):
            for m in range(unit):
                zz = r * unit + m
                own = jnp.logical_and(zz == z, core == t)
                send, recv, dev = zs_sem, zr_sem.at[src], at(q, t, zz)
                plain = remote(zsum.at[total_at(r, c, h, t, m)], z_recv.at[src, c, mine, h], send, recv, dev)
                flipped = remote(zsum.at[pl.ds(total_at(r, c, h, t), unit)], t_recv.at[src, :, mine, h], send, recv, dev)

                @pl.when(jnp.logical_and(own, jnp.logical_not(flip)))
                def _():
                    z_recv[0, c, mine, h] = zsum[total_at(r, c, h, t, m)]

                @pl.when(jnp.logical_and(own, flip))
                def _():
                    t_recv[0, :, mine, h] = zsum[pl.ds(total_at(r, c, h, t), unit)]

                @pl.when(jnp.logical_and(jnp.logical_not(own), jnp.logical_not(flip)))
                def _():
                    plain.start()

                @pl.when(jnp.logical_and(jnp.logical_not(own), flip))
                def _():
                    flipped.start()

    both = CORES * unit

    def sums_at(r, c, h):
        return pl.ds(total_at(r, c, h), both)

    def pair_copy(r, c, h, phase):
        return remote(zsum.at[sums_at(r, c, h)], pair.at[sums_at(lax.rem(r, mid), c, h)], qs_sem, qr_sem.at[phase],
                      at(q, core, z + unit - 2 * unit * half))

    def halfway(r, c, h):
        _, mine_f, mine_g = place(r, c, h)
        own = pl.ds(mine_f * side * CORES, side * CORES)
        total = portion[r, c, h, own]
        for d in range(side - 1):
            total = total + recv1[r, c, h, d]
        portion[r, c, h, own] = total
        for j in range(1, side):
            second_copy(r, c, h, lax.rem(mine_g + j, side)).start()

    def gather(r, c, h, phase):
        _, mine_f, mine_g = place(r, c, h)
        total = portion[r, c, h, pl.ds((mine_f * side + mine_g) * CORES, CORES)]
        for d in range(side - 1):
            total = total + recv2[r, c, h, d]
        zsum[sums_at(r, c, h)] = total.reshape(both, hr, cols)

        @pl.when(is_near(r))
        def _():
            deliver(r, c, h)

        @pl.when(jnp.logical_not(jnp.logical_or(is_near(r), inner)))
        def _():
            pair_copy(r, c, h, phase).start()

    def join(r, c, h):
        @pl.when(jnp.logical_not(is_near(r)))
        def _():
            zsum[sums_at(r, c, h)] = zsum[sums_at(r, c, h)] + pair[sums_at(lax.rem(r, mid), c, h)]
            deliver(r, c, h)

    def came(recv, sem, r, c, h=None):
        for d in range(side - 1):
            ref = recv.at[r, c, :, d] if h is None else recv.at[0, pl.ds(0, 2), 0, d]
            arrived(ref, sem.at[*(mark(r, c, h) if h is not None else (r, c)), d])

    def over(do, i, recv=None, sem=None):
        def one(j, carry):
            r, c = item(i, j)
            if sem is not None:
                came(recv, sem, r, c)
            for h in range(pieces):
                do(r, c, h)
            return carry

        lax.fori_loop(0, 2 * i + 1, one, 0)

    def over_last(do, h, recv=None, sem=None):
        def one(j, carry):
            a = order(j)
            if sem is not None:
                came(recv, sem, far_outer, a, h)
            do(far_outer, a, h)
            do(a, far_outer, h)
            return carry

        lax.fori_loop(0, last, one, 0)

    def over_corner(do, recv=None, sem=None):
        if sem is not None:
            came(recv, sem, far_outer, far_outer)
        for h in range(pieces):
            do(far_outer, far_outer, h)

    def in_phase(phase):
        return lambda r, c, h: gather(r, c, h, phase)

    def joined(phase, count, run):
        @pl.when(inner)
        def _():
            arrived(pair.at[pl.ds(0, count * both)], qr_sem.at[phase])
            run()

    step(0)
    step(1)
    pl.when(far_inner)(lambda: pass_on(ahead))
    over(halfway, 0, recv1, xr1_sem)
    over(halfway, 1, recv1, xr1_sem)
    step(2)
    pl.when(far_inner)(lambda: pass_on(relay_list[len(ahead):]))
    over(in_phase(0), 0, recv2, xr2_sem)
    over(in_phase(0), 1, recv2, xr2_sem)
    for h in range(pieces - 1):
        last_step(h)
        over(halfway, 2, recv1, xr1_sem)
        over_last(halfway, h, recv1, xr1_sem)
    if pieces == 1:
        over(halfway, 2, recv1, xr1_sem)
    last_step(pieces - 1, lambda: over(in_phase(0), 2, recv2, xr2_sem))
    joined(0, last * pieces, lambda: over(join, 2))
    block(far_outer, far_outer)
    for h in range(pieces - 1):
        over_last(in_phase(1 + h), h, recv2, xr2_sem)
    over_last(halfway, pieces - 1, recv1, xr1_sem)
    for h in range(pieces - 1):
        joined(1 + h, last + 1, lambda h=h: over_last(join, h))
    over_corner(halfway, recv1, xr1_sem)
    over_last(in_phase(pieces), pieces - 1, recv2, xr2_sem)
    joined(pieces, last + 1, lambda: over_last(join, pieces - 1))
    over_corner(in_phase(pieces + 1), recv2, xr2_sem)
    joined(pieces + 1, pieces, lambda: over_corner(join))

    one_each = last + unit
    pl.when(far_sender)(lambda: arrived(f_full.at[:, 0], fs_sem))
    pl.when(jnp.logical_not(far_sender))(lambda: arrived(f_full.at[pl.ds(0, n - 1), 0], fs_sem))
    pl.when(far_sender)(lambda: arrived(relay, ps_sem))
    pl.when(jnp.logical_not(far_sender))(lambda: arrived(relay.at[pl.ds(0, (n - 1) * pieces)], ps_sem))
    pl.when(far_inner)(lambda: arrived(relay, rf_sem))
    arrived(f_full.at[:, others], f2s_sem)
    arrived(s_full.at[:, :, others], ss_sem)
    arrived(recv1, xs1_sem)
    arrived(recv2, xs2_sem)
    near_count = pieces * one_each * (mid * both - 1)
    far_count = pieces * both * (one_each + (mid - 1) * units)
    pl.when(inner)(lambda: arrived(zsum.at[pl.ds(0, near_count + far_count)], zs_sem))

    @pl.when(jnp.logical_not(inner))
    def _():
        arrived(zsum.at[pl.ds(0, near_count)], zs_sem)
        arrived(pair, qs_sem)

    anc_copy.wait()
    row0 = pl.multiple_of(lax.rem(z, unit) * rows_z, rows_z)
    for src in range(SOURCES):
        count = pieces * one_each * (split if src else split - 1)
        if src < SOURCES - 1:
            arrived(zsum.at[pl.ds(0, count)], zr_sem.at[src])
        else:
            pl.when(inner)(lambda: arrived(zsum.at[pl.ds(0, count)], zr_sem.at[src]))
            pl.when(jnp.logical_not(inner))(
                lambda: arrived(zsum.at[pl.ds(0, pieces * units * split)], zr_sem.at[src]))
        outermost = far_outer if src < SOURCES - 1 else outer_unit
        for c in range(units):
            flip = outermost == c
            if src == SOURCES - 1:
                flip = jnp.logical_and(flip, inner)

            @pl.when(flip)
            def _():
                turned[...] = t_recv[src].reshape(cols, cols).T
                out[0, :, c * cols:(c + 1) * cols] = (
                    out[0, :, c * cols:(c + 1) * cols] - turned[pl.ds(row0, rows_z)])

            @pl.when(jnp.logical_not(flip))
            def _():
                out[0, :, c * cols:(c + 1) * cols] = (
                    out[0, :, c * cols:(c + 1) * cols] - z_recv[src, c].reshape(rows_z, cols))


def shards(panels, factors, member, target, ancestors):
    sups, blk_count, nb = factors.shape[0], panels.shape[0], member.shape[1]
    width = panels.shape[2]
    n, wide_count = lax.axis_size("narrow"), lax.axis_size("wide")
    side = math.isqrt(wide_count // CORES)
    assert side * side * CORES == wide_count
    tile_count = ancestors.shape[0] * wide_count
    assert ancestors.shape[0] == 1 and n % (CORES * sups) == 0 and nb % 2 == 0 and sups == 2
    assert blk_count == sups * nb
    unit = n // (CORES * sups)
    split = unit * CORES
    part = panels.shape[1] // split
    pieces = max(1, part // PIECE)
    assert pieces <= 2 and n == sups * split
    hr = part // pieces
    units = CORES * sups
    cols = width // units
    f32, bf16 = jnp.float32, jnp.bfloat16
    dma = pltpu.SemaphoreType.DMA
    cfg = (n, side, sups, nb, width, part, unit, split, pieces)
    any_space = pl.BlockSpec(memory_space=pl.ANY)
    smem = pl.BlockSpec(memory_space=pltpu.SMEM)
    return pl.pallas_call(
        functools.partial(kernel, cfg),
        out_shape=jax.ShapeDtypeStruct(ancestors.shape, f32),
        in_specs=[smem, smem, any_space, any_space, any_space],
        out_specs=pl.BlockSpec(memory_space=pltpu.VMEM),
        scratch_shapes=[
            pltpu.VMEM(panels.shape, f32),
            pltpu.VMEM((sups, nb, panels.shape[1], width), f32),
            pltpu.VMEM((n, pieces, nb, hr, width), f32),
            pltpu.VMEM((n, split, part, width), f32),
            pltpu.VMEM((width, width), bf16),
            pltpu.VMEM((width, width), bf16),
            pltpu.VMEM((nb, n, split, part, width), f32),
            pltpu.VMEM((nb, n, split, part, width), bf16),
            pltpu.VMEM((nb, n, split, part, width), bf16),
            pltpu.VMEM((nb * unit * part, nb * cols), f32),
            pltpu.VMEM((units, units, pieces, tile_count, unit, hr, cols), f32),
            pltpu.VMEM((units, units, pieces, side - 1, side * CORES, unit, hr, cols), f32),
            pltpu.VMEM((units, units, pieces, side - 1, CORES, unit, hr, cols), f32),
            pltpu.VMEM((units * units * pieces * CORES * unit * unit, hr, cols), f32),
            pltpu.VMEM((units // 2 * units * pieces * CORES * unit, hr, cols), f32),
            pltpu.VMEM((SOURCES, units, split, pieces, hr, cols), f32),
            pltpu.VMEM((SOURCES, unit, split, pieces, hr, cols), f32),
            pltpu.VMEM((cols, cols), f32),
            pltpu.VMEM((sups * split * pieces, nb, hr, width), f32),
            dma, dma,
            dma, dma,
            dma, dma,
            dma, dma((n, pieces)),
            dma, dma((n, pieces)),
            dma, dma((units, units, side - 1)),
            dma, dma((units, units, side - 1)),
            dma, dma((SOURCES,)),
            dma, dma((pieces + 2,)),
            dma((sups * split * pieces,)), dma,
        ],
        compiler_params=pltpu.CompilerParams(
            collective_id=0, has_side_effects=True, vmem_limit_bytes=58 * 2**20
        ),
        name="level",
    )(member, target, panels, factors, ancestors)


def solution(mesh):
    return jax.shard_map(
        shards,
        mesh=mesh,
        in_specs=(
            P("wide", "narrow", None),
            P("wide", "narrow", None),
            P(),
            P(),
            P("wide", "narrow", None),
        ),
        out_specs=P("wide", "narrow", None),
        check_vma=False,
    )
```

time: 118 us -> 87.4 us (0.74)
  Pallas kernels: 115 us -> 84 us
    pallas_call x1, Pallas kernels: 115 us -> 84 us  [shards(): pl.pallas_call(functools.partial(kernel, cfg), out_shape=jax.ShapeDtypeSt...]
where the time goes in v2:
time: 87.4 us; the launch traced here: 87.1 us
  Pallas kernels  84 us (96%)
  local copies, waits for them, and re-layouts  3.03 us (3%)
    pallas_call x1, Pallas kernels, shards(): pl.pallas_call(functools.partial(kernel, cfg), out_shape=jax.ShapeDtypeSt...  84 us
    unnamed x2, local copies, waits for them, and re-layouts  3.03 us

profile of v2, /device:TPU:0, one launch (start us, length us, event | category | flops | bytes accessed | tf_op | source)
XLA Modules:
  0.0 87.1 jit_solution(6149025315896165797)
XLA Ops:
  0.0 1.4 %copy.6.member = s32[16,4]{1,0:T(8,128)} copy(s32[16,4]{0,1:T(4,128)} %param.7) | data formatting | bytes 512 | tf_op args[2]
  1.4 84.0 %level.1 = f32[1,128,512]{2,1,0:T(8,128)} custom-call(s32[16,4]{1,0:T(8,128)} %copy.6.member, s32[16,10]{1,0:T(8,128)} %target.1, f32[8,128,512]{2,1,0:T(8,128)} %panels.1, f32[2,128,512]{2,1,0:T(8,128)} %factors.1, f32[1,128,512]{2,1,0:T(8,128)} %ancestors.1), custom_call_target="tpu_custom_call" | custom-call | tf_op jit(solution)/shard_map/level/pallas_call | solution.py:548
  85.4 1.7 %copy.8 = f32[1,128,512]{2,1,0:T(8,128)} copy(f32[1,128,512]{2,1,0:T(8,128)} %level.1) | data formatting | bytes 524288

commit v3 on v2

--- a/solution.py
+++ b/solution.py
@@ -122,7 +122,7 @@
 
     def pick(i, carry):
         s, k = lax.div(i, nb), lax.rem(i, nb)
-        stage[s, k] = pan[lax.rem(member[wide * sups + s, k], sups * nb)]
+        stage[s, k] = pan[lax.rem(member[k, wide * sups + s], sups * nb)]
         return carry
 
     lax.fori_loop(0, sups * nb, pick, 0)
@@ -131,7 +131,7 @@
     far_outer_sender = jnp.logical_and(far_sender, jnp.logical_not(inner))
     p_list = [(i, e, h) for i in range(sups) for h in range(pieces) for e in range(split)]
     relay_list = [(i, e, h) for h in range(pieces) for i in reversed(range(sups)) for e in range(split)]
-    ahead = relay_list[:sups * split * max(1, pieces // 2)]
+    quarter = len(relay_list) // 4
 
     def slot(s, e, h):
         return (s * split + e) * pieces + h
@@ -449,18 +449,21 @@
 
     step(0)
     step(1)
-    pl.when(far_inner)(lambda: pass_on(ahead))
+    pl.when(far_inner)(lambda: pass_on(relay_list[:2 * quarter]))
     over(halfway, 0, recv1, xr1_sem)
     over(halfway, 1, recv1, xr1_sem)
     step(2)
-    pl.when(far_inner)(lambda: pass_on(relay_list[len(ahead):]))
+    pl.when(far_inner)(lambda: pass_on(relay_list[2 * quarter:3 * quarter]))
     over(in_phase(0), 0, recv2, xr2_sem)
     over(in_phase(0), 1, recv2, xr2_sem)
     for h in range(pieces - 1):
         last_step(h)
+        if h == 0:
+            pl.when(far_inner)(lambda: pass_on(relay_list[3 * quarter:]))
         over(halfway, 2, recv1, xr1_sem)
         over_last(halfway, h, recv1, xr1_sem)
     if pieces == 1:
+        pl.when(far_inner)(lambda: pass_on(relay_list[3 * quarter:]))
         over(halfway, 2, recv1, xr1_sem)
     last_step(pieces - 1, lambda: over(in_phase(0), 2, recv2, xr2_sem))
     joined(0, last * pieces, lambda: over(join, 2))
@@ -582,10 +585,10 @@
             dma((sups * split * pieces,)), dma,
         ],
         compiler_params=pltpu.CompilerParams(
-            collective_id=0, has_side_effects=True, vmem_limit_bytes=58 * 2**20
+            collective_id=0, has_side_effects=True, vmem_limit_bytes=54912 * 2**10
         ),
         name="level",
-    )(member, target, panels, factors, ancestors)
+    )(member.T, target, panels, factors, ancestors)
 
 
 def solution(mesh):

time: 87.4 us -> 85.4 us (0.977)
  local copies, waits for them, and re-layouts: 3.03 us -> 2.08 us
  Pallas kernels: 84 us -> 83.1 us
    unnamed x2 -> x5, local copies, waits for them, and re-layouts: 3.03 us -> 2.08 us
    pallas_call x1, Pallas kernels: 84 us -> 83.1 us  [shards(): pl.pallas_call(functools.partial(kernel, cfg), out_shape=jax.ShapeDtypeSt...]
where the time goes in v3:
time: 85.4 us; the launch traced here: 85.2 us
  Pallas kernels  83.1 us (97%)
  local copies, waits for them, and re-layouts  2.08 us (2%)
    pallas_call x1, Pallas kernels, shards(): pl.pallas_call(functools.partial(kernel, cfg), out_shape=jax.ShapeDtypeSt...  83.1 us
    unnamed x5, local copies, waits for them, and re-layouts  2.08 us

profile of v3, /device:TPU:0, one launch (start us, length us, event | category | flops | bytes accessed | tf_op | source)
XLA Modules:
  0.0 85.2 jit_solution(7502913058549656411)
XLA Ops:
  0.0 0.0 copy-start
  0.0 0.7 copy-done
  0.7 0.0 copy-start.1
  0.7 0.7 copy-done.1
  1.4 83.1 %level.1 = f32[1,128,512]{2,1,0:T(8,128)S(1)} custom-call(s32[4,16]{1,0:T(4,128)S(1)} %bitcast.1, s32[16,10]{1,0:T(8,128)S(1)} %copy-done, f32[8,128,512]{2,1,0:T(8,128)} %panels.1, f32[2,128,512]{2,1,0:T(8,128)} %factors.1, f32[1,128,512]{2,1,0:T(8,128)} %ancestors.1), custom_call_target="tpu_custom_call" | custom-call | tf_op jit(solution)/shard_map/level/pallas_call | solution.py:551
  84.5 0.7 copy.7
Async XLA Ops:
  0.0 0.7 copy-start
  0.7 0.7 copy-start.1
